TPU v7x, 128 devices: a whole 4x4x4 slice. The times are simulated.
128 devices in a mesh: freq: 8 (over x, z_hi), panel: 16 (over z_lo, y, core).
Axes of the slice: x: 4, y: 4, z: 4 (z_hi: 2, z_lo: 2; z = z_hi * 2 + z_lo), core: 2. Of those that a mesh axis runs over, the one named last changes fastest.
Arguments:
- traces: bfloat16 [640, 640, 1024], P('panel', 'freq'), may hold values from -6 to 6
- filters: float32 [16, 7, 64], replicated, may hold values from -0.25 to 0.25
Outputs:
- primaries: bfloat16 [640, 640, 1024], P('panel', 'freq')
All inputs are finite; a program needn't handle non-finite values.
Results may differ from a plain program's by a relative error of at most 0.0095.
Values may be sent and summed in bfloat16 or wider, within the bound.
No kernel may reach another device: no remote copies, remote signals or barrier semaphores. Data moves between devices by JAX's collectives and lax.ppermute only.
A program may use at most 128 MiB of HBM per device.

v0:
```python
import math
import jax
import jax.numpy as jnp
from jax import lax
from jax.sharding import PartitionSpec as P

NS = 640
NT = 1024
NF = 96
FLO = 8
TAPS = 64
SPAN = 7
RWIN = 40


def wave_table(freq_bins, sample_index):
    phases = freq_bins[:, None] * sample_index[None, :] % NT
    angles = phases.astype(jnp.float32) * jnp.float32(2.0 * math.pi / NT)
    return (jnp.cos(angles), jnp.sin(angles))


def complex_product(left_side, right_side):

    def factor_product(leading_factor, trailing_factor):
        return jnp.einsum(
            "gjo,god->gjd", leading_factor, trailing_factor, preferred_element_type=jnp.float32
        )

    part_real = factor_product(left_side[0], right_side[0]) - factor_product(
        left_side[1], right_side[1]
    )
    part_imag = factor_product(left_side[0], right_side[1]) + factor_product(
        left_side[1], right_side[0]
    )
    return jnp.stack([part_real, part_imag])


def response(filters, freq_bins):
    tap_index = jnp.arange(TAPS, dtype=jnp.int32)
    cosine_wave, sine_wave = wave_table(freq_bins, tap_index)
    filter_real = jnp.einsum("fk,wjk->fjw", cosine_wave, filters)
    filter_imag = -jnp.einsum("fk,wjk->fjw", sine_wave, filters)
    return (jnp.repeat(filter_real, RWIN, axis=2), jnp.repeat(filter_imag, RWIN, axis=2))


def apply_filter(extended, filter_real, filter_imag, source_count):
    sum_real = jnp.zeros(extended.shape[1:2] + (source_count,) + extended.shape[3:], jnp.float32)
    sum_imag = jnp.zeros_like(sum_real)
    for shifted in range(SPAN):
        part_real = extended[0, :, shifted : shifted + source_count, :]
        part_imag = extended[1, :, shifted : shifted + source_count, :]
        weight_real = filter_real[:, shifted][:, None, :]
        weight_imaginary = filter_imag[:, shifted][:, None, :]
        sum_real = sum_real + weight_real * part_real - weight_imaginary * part_imag
        sum_imag = sum_imag + weight_real * part_imag + weight_imaginary * part_real
    return jnp.stack([sum_real, sum_imag])


def per_device(traces, filters):
    shot_rows, receiver_cols, time_sample_count = traces.shape
    rim_width = SPAN // 2
    scale_sources = jnp.float32(math.sqrt(NS))
    freq_bins = FLO + jnp.arange(NF, dtype=jnp.int32)
    cosine_wave, sine_wave = wave_table(freq_bins, jnp.arange(NT, dtype=jnp.int32))
    forward = (jnp.concatenate([cosine_wave, -sine_wave], 0) / jnp.float32(math.sqrt(NT))).astype(
        jnp.bfloat16
    )
    reciprocal_value = jnp.concatenate([cosine_wave, -sine_wave], 0).astype(jnp.bfloat16)
    spectra = jnp.einsum("srt,ct->csr", traces, forward, preferred_element_type=jnp.float32)
    spectra = spectra.astype(jnp.bfloat16).reshape(2, NF, shot_rows, receiver_cols)
    columns = lax.all_to_all(spectra, "panel", split_axis=1, concat_axis=2, tiled=True)
    slice_count = columns.shape[1]
    first_slice = lax.axis_index("panel") * slice_count
    complete = lax.all_gather(columns, "freq", axis=3, tiled=True)
    order_one = (complex_product(complete, columns) / scale_sources).astype(jnp.bfloat16)
    order_two = complex_product(complete, order_one) / scale_sources
    prediction = (order_one.astype(jnp.float32) - order_two).astype(jnp.bfloat16)
    extended = jnp.pad(
        prediction.astype(jnp.float32), ((0, 0), (0, 0), (rim_width, rim_width), (0, 0))
    )
    own_bins = FLO + first_slice + jnp.arange(slice_count, dtype=jnp.int32)
    filter_real, filter_imag = response(filters, own_bins)
    receiver_start = lax.axis_index("freq") * receiver_cols
    filter_real = lax.dynamic_slice_in_dim(filter_real, receiver_start, receiver_cols, 2)
    filter_imag = lax.dynamic_slice_in_dim(filter_imag, receiver_start, receiver_cols, 2)
    matched = apply_filter(extended, filter_real, filter_imag, NS)
    returned = lax.all_to_all(
        matched.astype(jnp.bfloat16), "panel", split_axis=2, concat_axis=1, tiled=True
    )
    matched_rows = returned.reshape(2 * NF, shot_rows, receiver_cols)
    multiples = jnp.einsum(
        "csr,ct->srt", matched_rows, reciprocal_value, preferred_element_type=jnp.float32
    )
    multiples = multiples / jnp.float32(math.sqrt(NF))
    return (traces.astype(jnp.float32) - multiples).astype(jnp.bfloat16)


def solution(mesh):
    placed = (P("panel", "freq", None), P())
    return jax.shard_map(
        per_device, mesh=mesh, in_specs=placed, out_specs=P("panel", "freq", None), check_vma=False
    )
```

profile of v0, /device:TPU:1, one launch (start us, length us, event | category | flops | bytes accessed | tf_op | source)
XLA Modules:
  0.0 312.2 jit_solution(14349941599640643925)
XLA Ops:
  6.5 0.0 copy-start
  6.5 0.0 all-gather.2.cloned.1.call-start
  6.5 1.6 fusion.58
  8.2 0.0 copy-start.4
  8.2 0.0 copy-start.6
  8.2 0.8 copy-done.4
  8.9 0.2 copy-done.6
  9.1 4.8 %convolution_convert_fusion = bf16[192,40,80]{0,2,1:T(8,128)(2,1)S(1)} fusion(bf16[40,80,1024]{2,1,0:T(8,128)(2,1)} %param.2, f32[96,1024]{1,0:T(8,128)S(1)} %get-tuple-element.24, f32[96,1024]{1,0:T(8,128)S(1)} %get-tuple-element.23), kind=kOutput, calls=%fused_computation.35 | convolution fusion | flops 1259495424 | bytes 8568832 | tf_op jit(solution)/shard_map/srt,ct->csr/dot_general | solution.py:69
  13.9 0.9 reshape.26
  14.7 3.3 %copy.54 = bf16[2,96,40,80]{3,2,0,1:T(8,128)(2,1)} copy(bf16[2,96,40,80]{1,0,3,2:T(2,128)(2,1)S(1)} %reshape.26) | data formatting | bytes 2457600 | tf_op jit(solution)/shard_map/reshape | solution.py:70
  18.1 32.3 %all_to_all.33 = bf16[2,96,40,80]{3,2,0,1:T(8,128)(2,1)S(1)} all-to-all(bf16[2,96,40,80]{3,2,0,1:T(8,128)(2,1)} %copy.54), channel_id=1, replica_groups=mesh['freq'=8,'panel'=16] {'panel'}, dimensions={1} | all-to-all | bytes 2457600 | tf_op jit(solution)/shard_map/all_to_all | solution.py:71
  50.4 1.7 copy.56
  52.2 4.5 %copy.57 = bf16[2,6,640,80]{2,0,1,3:T(2,128)(2,1)} copy(bf16[2,6,640,80]{3,2,1,0:T(8,128)(2,1)} %bitcast.140) | data formatting | bytes 2457600 | tf_op jit(solution)/shard_map/all_to_all | solution.py:71
  56.7 0.0 all-gather.2.cloned.1.call-update
  56.7 0.0 copy-done
  56.8 0.2 convolution_bitcast_fusion
  57.0 0.2 broadcast_in_dim.4
  57.2 0.2 reshape.25
  57.4 0.2 fusion.45
  57.7 0.2 broadcast_in_dim.5
  57.8 0.2 reshape.27
  58.1 0.2 constant_dynamic-slice_fusion.10
  58.4 0.3 copy.55
  58.7 0.3 fusion.81
  59.1 0.1 copy.62
  59.2 0.1 copy.59
  59.3 118.6 %all-gather.2.cloned.1.call-done = bf16[2,6,640,640]{2,0,1,3:T(2,128)(2,1)} async-done(((bf16[2,6,640,80]{2,0,1,3:T(2,128)(2,1)}), bf16[2,6,640,640]{2,0,1,3:T(2,128)(2,1)}) %all-gather.2.cloned.1.call-update) | async-done | bytes 9830416 | tf_op jit(solution)/shard_map/all_gather | solution.py:74
  177.9 20.6 %fusion.80 = (bf16[1,6,640,640]{2,0,1,3:T(2,128)(2,1)}, bf16[1,6,640,640]{2,0,1,3:T(2,128)(2,1)}) fusion(bf16[2,6,640,640]{2,0,1,3:T(2,128)(2,1)} %all-gather.2.cloned.1.call-done), kind=kLoop, calls=%fused_computation.122 | loop fusion | bytes 19660800 | tf_op jit(solution)/shard_map/slice | solution.py:29
  198.5 19.7 %copy.91 = bf16[1,6,640,640]{3,2,1,0:T(8,128)(2,1)} copy(bf16[1,6,640,640]{2,0,1,3:T(2,128)(2,1)} %get-tuple-element.6) | data formatting | bytes 9830400
  218.3 19.8 %copy.90 = bf16[1,6,640,640]{3,2,1,0:T(8,128)(2,1)} copy(bf16[1,6,640,640]{2,0,1,3:T(2,128)(2,1)} %get-tuple-element.5) | data formatting | bytes 9830400
  238.0 0.0 copy-start.2
  238.0 4.2 %fusion.6 = f32[6,640,80]{1,2,0:T(8,128)S(1)} fusion(bf16[6,640,80]{2,1,0:T(8,128)(2,1)S(1)} %bitcast.133, bf16[1,6,640,640]{3,2,1,0:T(8,128)(2,1)} %copy.91), kind=kOutput, calls=%fused_computation.7 | convolution fusion | flops 393216000 | bytes 6758400 | tf_op jit(solution)/shard_map/gjo,god->gjd/dot_general | solution.py:25
  242.2 0.0 copy-done.2
  242.2 0.0 copy-start.3
  242.2 1.7 fusion.4
  243.9 0.7 copy-done.3
  244.6 1.7 fusion.23
  246.3 1.7 fusion.29
  247.9 0.2 fusion.16
  248.2 1.7 fusion.2
  249.8 1.7 fusion
  251.5 1.7 fusion.35
  253.2 1.7 fusion.41
  254.8 0.4 fusion.44
  255.2 5.4 %subtract_convert_fusion.1 = bf16[1,6,640,80]{2,3,1,0:T(8,128)(2,1)S(1)} fusion(f32[2,6,640,80]{2,3,1,0:T(8,128)S(1)} %fusion.44, f32[6,80]{1,0:T(8,128)S(1)} %bitcast.143, f32[6,80]{1,0:T(8,128)S(1)} %bitcast.145, f32[6,80]{1,0:T(8,128)S(1)} %bitcast.147, f32[6,80]{1,0:T(8,128)S(1)} %bitcast.149, f32[6,80]{1,0:T(8,128)S(1)} %bitcast.151, ...), kind=kLoop, calls=%fused_computation.47 | loop fusion | flops 8601600 | bytes 5586944 | tf_op jit(solution)/shard_map/convert
  260.6 5.3 %add_convert_fusion = bf16[1,6,640,80]{2,3,1,0:T(8,128)(2,1)S(1)} fusion(f32[2,6,640,80]{2,3,1,0:T(8,128)S(1)} %fusion.44, f32[6,80]{1,0:T(8,128)S(1)} %bitcast.144, f32[6,80]{1,0:T(8,128)S(1)} %bitcast.146, f32[6,80]{1,0:T(8,128)S(1)} %bitcast.148, f32[6,80]{1,0:T(8,128)S(1)} %bitcast.150, f32[6,80]{1,0:T(8,128)S(1)} %bitcast.152, ...), kind=kLoop, calls=%fused_computation.46 | loop fusion | flops 8601600 | bytes 5586944 | tf_op jit(solution)/shard_map/convert.1
  265.9 0.1 pad_maximum_fusion
  266.1 2.6 copy.67
  268.6 0.0 slice-start
  268.7 30.9 %all_to_all.34 = bf16[2,6,640,80]{3,0,1,2:T(2,128)(2,1)S(1)} all-to-all(bf16[2,6,640,80]{3,0,1,2:T(2,128)(2,1)S(1)} %copy.67), channel_id=1, replica_groups=mesh['freq'=8,'panel'=16] {'panel'}, dimensions={2} | all-to-all | bytes 2457600 | tf_op jit(solution)/shard_map/all_to_all | solution.py:87
  299.5 0.0 slice-start.1
  299.5 0.4 copy.68
  299.9 0.0 copy-start.5
  299.9 0.0 copy-start.7
  299.9 0.3 copy.69
  300.3 0.0 slice-done
  300.3 0.9 slice-done.1
  301.2 0.1 copy-done.5
  301.3 0.1 copy-done.7
  301.4 0.0 copy-start.1
  301.4 4.0 %subtract_convert_fusion = bf16[40,80,1024]{2,1,0:T(8,128)(2,1)} fusion(bf16[40,80,1024]{2,1,0:T(8,128)(2,1)S(1)} %bitcast.142, bf16[192,40,80]{2,1,0:T(8,128)(2,1)S(1)} %bitcast.138, f32[96,1024]{1,0:T(8,128)S(1)} %copy-done.7, f32[96,1024]{1,0:T(8,128)S(1)} %copy-done.5), kind=kOutput, calls=%fused_computation | convolution fusion | flops 1272184832 | bytes 15122432 | tf_op jit(solution)/shard_map/csr,ct->srt/dot_general | solution.py:91
  305.4 0.0 copy-done.1
  (19 shorter events, 0.1 us)
Async XLA Ops:
  6.5 50.2 %copy-start = (f32[16,7,64]{2,0,1:T(8,128)S(1)}, f32[16,7,64]{2,0,1:T(8,128)}, u32[]{:S(2)}) copy-start(f32[16,7,64]{2,0,1:T(8,128)} %param.3) | copy-start | bytes 86020
  6.5 171.3 %all-gather.2.cloned.1.call-start = ((), (), s32[]{:S(2)}) async-start(), calls=%async_computation.2 | async-start | bytes 11059200 | tf_op jit(solution)/shard_map/all_gather | solution.py:74
  8.2 0.8 copy-start.4
  8.2 0.9 copy-start.6
  238.0 4.2 %copy-start.2 = (bf16[1,6,640,640]{3,2,1,0:T(8,128)(2,1)S(1)}, bf16[1,6,640,640]{3,2,1,0:T(8,128)(2,1)}, u32[]{:S(2)}) copy-start(bf16[1,6,640,640]{3,2,1,0:T(8,128)(2,1)} %copy.91) | copy-start | bytes 14745604
  242.2 2.4 copy-start.3
  268.6 31.6 %slice-start = ((s8[6553600]{0:T(1024)(128)(4,1)}), s8[4194304]{0:T(1024)(128)(4,1)S(1)}, s32[]{:S(2)}) async-start(s8[6553600]{0:T(1024)(128)(4,1)} %bitcast.141), calls=%async_computation.3 | async-start | bytes 8388608
  299.5 1.7 slice-start.1
  299.9 1.4 copy-start.5
  299.9 1.5 copy-start.7
  301.4 4.0 %copy-start.1 = (f32[16,7,64]{2,0,1:T(8,128)S(1)}, f32[16,7,64]{2,0,1:T(8,128)}, u32[]{:S(2)}) copy-start(f32[16,7,64]{2,0,1:T(8,128)} %param.3) | copy-start | bytes 86020
Sparse Core Ops, SparseCore 0:
  56.8 120.9 all-gather.1
where the time goes:
time: 314 us; the launch traced here: 312 us
  waiting for transfers between devices  119 us (38%)
  local copies, waits for them, and re-layouts  78.6 us (25%)
  blocking collectives  63.2 us (20%)
  matrix products  25 us (8%)
  between operations  13.7 us (4%)
  other arithmetic  13.1 us (4%)
    all_gather x1, waiting for transfers between devices, per_device(): complete = lax.all_gather(columns, 'freq', axis=3, tiled=True)  119 us
    unnamed x36, local copies, waits for them, and re-layouts  42.4 us
    all_to_all x1, blocking collectives, per_device(): lax.all_to_all(spectra, 'panel', split_axis=1, concat_axis=2, tiled=True)  32.3 us
    all_to_all x1, blocking collectives, per_device(): lax.all_to_all(matched.astype(jnp.bfloat16), 'panel', split_axis=2, conca...  30.9 us
    slice x1, local copies, waits for them, and re-layouts, complex_product(): left_side[0]  20.6 us
    dot_general x8, matrix products, factor_product(): jnp.einsum('gjo,god->gjd', leading_factor, trailing_factor, preferred_ele...  15.8 us
    another operation x2, other arithmetic  10.7 us
    all_to_all x3, local copies, waits for them, and re-layouts, per_device(): lax.all_to_all(spectra, 'panel', split_axis=1, concat_axis=2, tiled=True)  6.6 us
  transfers between devices with their start and end apart: 1, of which 1 were waited for; matrix products, arithmetic and copies ran while one was open for 1% of the time, Pallas kernels for 0%

commit v1 on v0

--- a/solution.py
+++ b/solution.py
@@ -84,8 +84,14 @@
     filter_real = lax.dynamic_slice_in_dim(filter_real, receiver_start, receiver_cols, 2)
     filter_imag = lax.dynamic_slice_in_dim(filter_imag, receiver_start, receiver_cols, 2)
     matched = apply_filter(extended, filter_real, filter_imag, NS)
-    returned = lax.all_to_all(
-        matched.astype(jnp.bfloat16), "panel", split_axis=2, concat_axis=1, tiled=True
+    returned = jnp.concatenate(
+        jax.lax.all_to_all(
+            jnp.stack(jnp.split(matched.astype(jnp.bfloat16), jax.lax.axis_size("panel"), axis=2)),
+            "panel",
+            0,
+            0,
+        ),
+        axis=1,
     )
     matched_rows = returned.reshape(2 * NF, shot_rows, receiver_cols)
     multiples = jnp.einsum(

time: 314 us -> 329 us (1.048)
  other arithmetic: 13.1 us -> 26.5 us
    unnamed x1 -> x15, other arithmetic: 0.01 us -> 12.4 us
    unnamed x36 -> x32, local copies, waits for them, and re-layouts: 42.4 us -> 42 us
where the time goes in v1:
time: 329 us; the launch traced here: 327 us
  waiting for transfers between devices  119 us (36%)
  local copies, waits for them, and re-layouts  78.7 us (24%)
  blocking collectives  63 us (19%)
  matrix products  26.9 us (8%)
  other arithmetic  26.5 us (8%)
  between operations  13.7 us (4%)
    all_gather x1, waiting for transfers between devices, per_device(): complete = lax.all_gather(columns, 'freq', axis=3, tiled=True)  119 us
    unnamed x32, local copies, waits for them, and re-layouts  42 us
    all_to_all x1, blocking collectives, per_device(): lax.all_to_all(spectra, 'panel', split_axis=1, concat_axis=2, tiled=True)  32.3 us
    all_to_all x1, blocking collectives, per_device(): jax.lax.all_to_all(jnp.stack(jnp.split(matched.astype(jnp.bfloat16), jax....  30.6 us
    slice x1, local copies, waits for them, and re-layouts, complex_product(): left_side[0]  20.5 us
    dot_general x8, matrix products, factor_product(): jnp.einsum('gjo,god->gjd', leading_factor, trailing_factor, preferred_ele...  15.8 us
    unnamed x15, other arithmetic  12.4 us
    another operation x2, other arithmetic  10.9 us
  transfers between devices with their start and end apart: 1, of which 1 were waited for; matrix products, arithmetic and copies ran while one was open for 1% of the time, Pallas kernels for 0%

profile of v1, /device:TPU:1, one launch (start us, length us, event | category | flops | bytes accessed | tf_op | source)
XLA Modules:
  0.0 327.4 jit_solution(3103156317381301593)
XLA Ops:
  6.5 0.0 copy-start
  6.5 1.6 fusion.105
  8.2 0.0 copy-start.4
  8.2 0.0 copy-start.6
  8.2 0.7 copy-done.4
  8.9 0.2 copy-done.6
  9.1 4.8 %convolution_convert_fusion = bf16[192,40,80]{0,2,1:T(8,128)(2,1)S(1)} fusion(bf16[40,80,1024]{2,1,0:T(8,128)(2,1)} %param.2, f32[96,1024]{1,0:T(8,128)S(1)} %get-tuple-element.24, f32[96,1024]{1,0:T(8,128)S(1)} %get-tuple-element.23), kind=kOutput, calls=%fused_computation.65 | convolution fusion | flops 1259495424 | bytes 8568832 | tf_op jit(solution)/shard_map/srt,ct->csr/dot_general | solution.py:69
  13.9 0.9 reshape.25
  14.7 3.3 %copy.33 = bf16[2,96,40,80]{3,2,0,1:T(8,128)(2,1)} copy(bf16[2,96,40,80]{1,0,3,2:T(2,128)(2,1)S(1)} %reshape.25) | data formatting | bytes 2457600 | tf_op jit(solution)/shard_map/reshape | solution.py:70
  18.1 32.3 %all_to_all.23 = bf16[2,96,40,80]{3,2,0,1:T(8,128)(2,1)S(1)} all-to-all(bf16[2,96,40,80]{3,2,0,1:T(8,128)(2,1)} %copy.33), channel_id=1, replica_groups=mesh['freq'=8,'panel'=16] {'panel'}, dimensions={1} | all-to-all | bytes 2457600 | tf_op jit(solution)/shard_map/all_to_all | solution.py:71
  50.4 1.7 copy.35
  52.2 4.5 %copy.36 = bf16[2,6,640,80]{2,0,1,3:T(2,128)(2,1)} copy(bf16[2,6,640,80]{3,2,1,0:T(8,128)(2,1)} %bitcast.202) | data formatting | bytes 2457600 | tf_op jit(solution)/shard_map/all_to_all | solution.py:71
  56.7 0.0 all-gather.2.cloned.1.call-update
  56.7 0.2 convolution_bitcast_fusion
  57.0 0.2 broadcast_in_dim.4
  57.2 0.2 reshape.24
  57.4 0.2 fusion.45
  57.6 0.2 broadcast_in_dim.5
  57.8 0.2 reshape.26
  58.0 0.2 constant_dynamic-slice_fusion.10
  58.4 0.3 copy.34
  58.7 0.3 fusion.128
  59.1 0.1 copy.41
  59.2 0.1 copy.38
  59.3 118.6 %all-gather.2.cloned.1.call-done = bf16[2,6,640,640]{2,0,1,3:T(2,128)(2,1)} async-done(((bf16[2,6,640,80]{2,0,1,3:T(2,128)(2,1)}), bf16[2,6,640,640]{2,0,1,3:T(2,128)(2,1)}) %all-gather.2.cloned.1.call-update) | async-done | bytes 9830416 | tf_op jit(solution)/shard_map/all_gather | solution.py:74
  177.9 20.5 %fusion.127 = (bf16[1,6,640,640]{2,0,1,3:T(2,128)(2,1)}, bf16[1,6,640,640]{2,0,1,3:T(2,128)(2,1)}) fusion(bf16[2,6,640,640]{2,0,1,3:T(2,128)(2,1)} %all-gather.2.cloned.1.call-done), kind=kLoop, calls=%fused_computation.199 | loop fusion | bytes 19660800 | tf_op jit(solution)/shard_map/slice | solution.py:29
  198.4 19.7 %copy.69 = bf16[1,6,640,640]{3,2,1,0:T(8,128)(2,1)} copy(bf16[1,6,640,640]{2,0,1,3:T(2,128)(2,1)} %get-tuple-element.6) | data formatting | bytes 9830400
  218.1 19.7 %copy.68 = bf16[1,6,640,640]{3,2,1,0:T(8,128)(2,1)} copy(bf16[1,6,640,640]{2,0,1,3:T(2,128)(2,1)} %get-tuple-element.5) | data formatting | bytes 9830400
  237.9 4.2 %fusion.6 = f32[6,640,80]{1,2,0:T(8,128)S(1)} fusion(bf16[6,640,80]{2,1,0:T(8,128)(2,1)S(1)} %bitcast.195, bf16[1,6,640,640]{3,2,1,0:T(8,128)(2,1)} %copy.69), kind=kOutput, calls=%fused_computation.7 | convolution fusion | flops 393216000 | bytes 6758400 | tf_op jit(solution)/shard_map/gjo,god->gjd/dot_general | solution.py:25
  242.1 0.0 copy-done.2
  242.1 1.7 fusion.4
  243.7 0.7 copy-done.3
  244.5 1.7 fusion.23
  246.1 1.7 fusion.29
  247.8 0.2 fusion.16
  248.0 1.7 fusion.2
  249.7 1.7 fusion
  251.3 1.7 fusion.35
  253.0 1.7 fusion.41
  254.7 0.5 fusion.44
  255.2 5.3 %add_convert_fusion = bf16[1,6,640,80]{2,3,1,0:T(8,128)(2,1)S(1)} fusion(f32[2,6,640,80]{2,3,1,0:T(8,128)S(1)} %fusion.44, f32[6,80]{1,0:T(8,128)S(1)} %bitcast.203, f32[6,80]{1,0:T(8,128)S(1)} %bitcast.205, f32[6,80]{1,0:T(8,128)S(1)} %bitcast.207, f32[6,80]{1,0:T(8,128)S(1)} %bitcast.209, f32[6,80]{1,0:T(8,128)S(1)} %bitcast.211, ...), kind=kLoop, calls=%fused_computation.75 | loop fusion | flops 8601600 | bytes 5586944 | tf_op jit(solution)/shard_map/convert.1
  260.5 5.6 %subtract_convert_fusion.1 = bf16[1,6,640,80]{2,3,1,0:T(8,128)(2,1)S(1)} fusion(f32[2,6,640,80]{2,3,1,0:T(8,128)S(1)} %fusion.44, f32[6,80]{1,0:T(8,128)S(1)} %bitcast.204, f32[6,80]{1,0:T(8,128)S(1)} %bitcast.206, f32[6,80]{1,0:T(8,128)S(1)} %bitcast.208, f32[6,80]{1,0:T(8,128)S(1)} %bitcast.210, f32[6,80]{1,0:T(8,128)S(1)} %bitcast.212, ...), kind=kLoop, calls=%fused_computation.76 | loop fusion | flops 8601600 | bytes 5586944 | tf_op jit(solution)/shard_map/convert
  266.1 0.7 fusion.63
  266.9 0.8 fusion.66
  267.7 0.8 fusion.69
  268.5 0.8 fusion.72
  269.4 0.8 fusion.75
  270.2 0.8 fusion.78
  271.0 0.8 fusion.81
  271.9 0.8 fusion.84
  272.7 0.8 fusion.87
  273.5 0.8 fusion.90
  274.4 0.8 fusion.93
  275.2 0.8 fusion.96
  276.0 0.8 fusion.99
  276.9 0.8 fusion.102
  277.7 0.8 fusion.60
  278.5 0.8 fusion.104
  279.3 3.6 %copy.46 = bf16[16,2,6,40,80]{4,3,2,1,0:T(8,128)(2,1)S(1)} copy(bf16[16,2,6,40,80]{3,4,2,1,0:T(8,128)(2,1)} %fusion.104) | data formatting | bytes 2457600 | tf_op jit(solution)/shard_map/stack | solution.py:89
  282.9 30.6 %all_to_all.24 = bf16[16,2,6,40,80]{4,3,2,1,0:T(8,128)(2,1)S(1)} all-to-all(bf16[16,2,6,40,80]{4,3,2,1,0:T(8,128)(2,1)S(1)} %copy.46), channel_id=1, replica_groups=mesh['freq'=8,'panel'=16] {'panel'}, dimensions={0} | all-to-all | bytes 2457600 | tf_op jit(solution)/shard_map/all_to_all | solution.py:88
  313.5 0.3 copy.47
  313.9 0.7 copy-done.5
  314.5 0.1 copy-done.7
  314.6 5.9 %subtract_convert_fusion = bf16[40,80,1024]{2,1,0:T(8,128)(2,1)} fusion(bf16[40,80,1024]{2,1,0:T(8,128)(2,1)} %param.2, bf16[192,40,80]{2,1,0:T(8,128)(2,1)S(1)} %bitcast.200, f32[96,1024]{1,0:T(8,128)S(1)} %copy-done.7, f32[96,1024]{1,0:T(8,128)S(1)} %copy-done.5), kind=kOutput, calls=%fused_computation | convolution fusion | flops 1272184832 | bytes 15122432 | tf_op jit(solution)/shard_map/csr,ct->srt/dot_general | solution.py:97
  (26 shorter events, 0.1 us)
Async XLA Ops:
  6.5 50.2 %copy-start = (f32[16,7,64]{2,0,1:T(8,128)S(1)}, f32[16,7,64]{2,0,1:T(8,128)}, u32[]{:S(2)}) copy-start(f32[16,7,64]{2,0,1:T(8,128)} %param.3) | copy-start | bytes 86020
  6.5 171.3 %all-gather.2.cloned.1.call-start = ((), (), s32[]{:S(2)}) async-start(), calls=%async_computation.2 | async-start | bytes 11059200 | tf_op jit(solution)/shard_map/all_gather | solution.py:74
  8.2 0.8 copy-start.4
  8.2 0.9 copy-start.6
  237.9 4.2 %copy-start.2 = (bf16[1,6,640,640]{3,2,1,0:T(8,128)(2,1)S(1)}, bf16[1,6,640,640]{3,2,1,0:T(8,128)(2,1)}, u32[]{:S(2)}) copy-start(bf16[1,6,640,640]{3,2,1,0:T(8,128)(2,1)} %copy.69) | copy-start | bytes 14745604
  242.1 2.4 copy-start.3
  313.5 1.0 copy-start.5
  313.5 1.1 copy-start.7
  314.6 5.9 %copy-start.1 = (f32[16,7,64]{2,0,1:T(8,128)S(1)}, f32[16,7,64]{2,0,1:T(8,128)}, u32[]{:S(2)}) copy-start(f32[16,7,64]{2,0,1:T(8,128)} %param.3) | copy-start | bytes 86020
Sparse Core Ops, SparseCore 0:
  56.8 120.9 all-gather.1
